TPU v7x, 32 devices: a whole 2x2x4 slice. The times are simulated.
32 devices in a mesh: groups: 2 (over y), axial: 16 (over z, x, core).
Axes of the slice: x: 2, y: 2, z: 4, core: 2. Of those that a mesh axis runs over, the one named last changes fastest.
Arguments:
- pair_rep: bfloat16 [192, 96, 128], P(('groups', 'axial')), parts along dimension 0, may hold values from -6 to 6
- norm_out: float32 [128], replicated, may hold values from 0.5 to 1.5
- proj_out: bfloat16 [128, 512], replicated, may hold values from -0.5 to 0.5
- gate_out: bfloat16 [128, 128], replicated, may hold values from -0.5 to 0.5
- mid_out: float32 [128], replicated, may hold values from 0.5 to 1.5
- final_out: bfloat16 [128, 128], replicated, may hold values from -0.5 to 0.5
- norm_in: float32 [128], replicated, may hold values from 0.5 to 1.5
- proj_in: bfloat16 [128, 512], replicated, may hold values from -0.5 to 0.5
- gate_in: bfloat16 [128, 128], replicated, may hold values from -0.5 to 0.5
- mid_in: float32 [128], replicated, may hold values from 0.5 to 1.5
- final_in: bfloat16 [128, 128], replicated, may hold values from -0.5 to 0.5
Outputs:
- updated: bfloat16 [192, 96, 128], P(('groups', 'axial')), parts along dimension 0
There are 2 independent parts, one for each index of `groups`. A program takes and returns all parts, laid end to end along the dimension named above; an argument that names none is the same for every part. Nothing has to cross between parts.
All inputs are finite; a program needn't handle non-finite values.
Results may differ from a plain program's by a relative error of at most 0.013.
Values may be sent and summed in bfloat16 or wider, within the bound.
A program may use at most 64 MiB of HBM per device.

v0:
```python
import jax
import jax.numpy as jnp
from jax import lax
from jax.sharding import PartitionSpec as P

EPS = 1e-05


def normalize(values, gain, axis):
    average = jnp.mean(values, axis=axis, keepdims=True)
    spread = jnp.mean(jnp.square(values - average), axis=axis, keepdims=True)
    return (values - average) * lax.rsqrt(spread + EPS) * gain


def channel_product(left_side, right_side, outgoing):
    formula = "kil,kjl->kij" if outgoing else "kli,klj->kij"
    got_left, got_right = (
        lax.all_to_all(left_side, "axial", split_axis=0, concat_axis=1, tiled=True),
        lax.all_to_all(right_side, "axial", split_axis=0, concat_axis=1, tiled=True),
    )
    return jnp.einsum(formula, got_left, got_right, preferred_element_type=jnp.float32)


def update(pair_rep, norm_gain, weights, gate_weight, mid_gain, final_weight, outgoing):
    normed = normalize(pair_rep.astype(jnp.float32), norm_gain, -1).astype(jnp.bfloat16)
    projected = jnp.einsum("rnc,ck->krn", normed, weights, preferred_element_type=jnp.float32)
    hidden = weights.shape[1] // 4
    left_side = (jax.nn.sigmoid(projected[hidden : 2 * hidden]) * projected[:hidden]).astype(
        jnp.bfloat16
    )
    right_side = (
        jax.nn.sigmoid(projected[3 * hidden :]) * projected[2 * hidden : 3 * hidden]
    ).astype(jnp.bfloat16)
    product = channel_product(left_side, right_side, outgoing)
    tri = lax.all_to_all(
        product.astype(jnp.bfloat16), "axial", split_axis=1, concat_axis=0, tiled=True
    )
    gating = jax.nn.sigmoid(
        jnp.einsum("rnc,ce->rne", normed, gate_weight, preferred_element_type=jnp.float32)
    )
    tri_normed = normalize(tri.astype(jnp.float32), mid_gain[:, None, None], 0).astype(jnp.bfloat16)
    result = jnp.einsum("krn,kc->rnc", tri_normed, final_weight, preferred_element_type=jnp.float32)
    return (pair_rep.astype(jnp.float32) + gating * result).astype(jnp.bfloat16)


def on_device(
    pair_rep,
    norm_out,
    proj_out,
    gate_out,
    mid_out,
    final_out,
    norm_in,
    proj_in,
    gate_in,
    mid_in,
    final_in,
):
    first = update(pair_rep, norm_out, proj_out, gate_out, mid_out, final_out, True)
    return update(first, norm_in, proj_in, gate_in, mid_in, final_in, False)


def solution(mesh):
    placed = (P(("groups", "axial"), None, None), P(), P(), P(), P(), P(), P(), P(), P(), P(), P())
    return jax.shard_map(
        on_device,
        mesh=mesh,
        in_specs=placed,
        out_specs=P(("groups", "axial"), None, None),
        check_vma=False,
    )
```

profile of v0, /device:TPU:0, one launch (start us, length us, event | category | flops | bytes accessed | tf_op | source)
XLA Modules:
  0.0 93.4 jit_solution(2439038225981949099)
XLA Ops:
  0.0 0.0 copy-start
  0.0 1.1 %convert_reduce_fusion = f32[6,96]{1,0:T(8,128)S(1)} fusion(bf16[6,96,128]{2,1,0:T(8,128)(2,1)} %param.11), kind=kLoop, calls=%fused_computation.20 | loop fusion | flops 146880 | bytes 149760 | tf_op jit(solution)/shard_map/reduce_sum | solution.py:10
  1.1 1.2 %fusion.19 = f32[6,96]{1,0:T(8,128)S(1)} fusion(bf16[6,96,128]{2,1,0:T(8,128)(2,1)} %param.11, f32[6,96]{1,0:T(8,128)S(1)} %broadcast_multiply_fusion.3), kind=kLoop, calls=%fused_computation.35 | loop fusion | flops 294336 | bytes 152064 | tf_op jit(solution)/shard_map/reduce_sum | solution.py:11
  2.3 0.0 copy-done
  2.3 1.3 %convolution_bitcast_fusion.1 = f32[512,6,96]{0,2,1:T(8,128)S(1)} fusion(bf16[128,512]{1,0:T(8,128)(2,1)S(1)} %copy-done, bf16[6,96,128]{2,1,0:T(8,128)(2,1)} %param.11, f32[128]{0:T(128)} %param.12, f32[6,96]{1,0:T(8,128)S(1)} %add_rsqrt_fusion.3, f32[6,96]{1,0:T(8,128)S(1)} %broadcast_multiply_fusion.3), kind=kOutput, calls=%fused_computation.1 | convolution fusion | flops 75866112 | bytes 1463296 | tf_op jit(solution)/shard_map/rnc,ck->krn/dot_general | solution.py:26
  3.6 0.2 fusion.34
  3.8 0.9 copy.39
  4.6 7.4 %all-to-all-start.1 = ((bf16[128,6,96]{2,1,0:T(8,128)(2,1)}), bf16[128,6,96]{2,1,0:T(8,128)(2,1)S(1)}, u32[]{:S(2)}, u32[]{:S(2)}) async-start(bf16[128,6,96]{2,1,0:T(8,128)(2,1)} %copy.39), calls=%async_computation.1 | async-start | bytes 524288 | tf_op jit(solution)/shard_map/all_to_all | solution.py:19
  12.0 0.9 copy.36
  12.9 9.1 %all-to-all-done.1 = bf16[128,6,96]{2,1,0:T(8,128)(2,1)S(1)} async-done(((bf16[128,6,96]{2,1,0:T(8,128)(2,1)}), bf16[128,6,96]{2,1,0:T(8,128)(2,1)S(1)}, u32[]{:S(2)}, u32[]{:S(2)}) %all-to-all-start.1) | async-done | bytes 147488 | tf_op jit(solution)/shard_map/all_to_all | solution.py:19
  22.1 3.5 %all-to-all-start = ((bf16[128,6,96]{2,1,0:T(8,128)(2,1)}), bf16[128,6,96]{2,1,0:T(8,128)(2,1)S(1)}, u32[]{:S(2)}, u32[]{:S(2)}) async-start(bf16[128,6,96]{2,1,0:T(8,128)(2,1)} %copy.36), calls=%async_computation | async-start | bytes 524288 | tf_op jit(solution)/shard_map/all_to_all | solution.py:18
  25.6 0.0 copy-start.1
  25.6 0.0 copy-start.7
  25.6 0.0 copy-start.9
  25.7 9.9 %all-to-all-done = bf16[128,6,96]{2,1,0:T(8,128)(2,1)S(1)} async-done(((bf16[128,6,96]{2,1,0:T(8,128)(2,1)}), bf16[128,6,96]{2,1,0:T(8,128)(2,1)S(1)}, u32[]{:S(2)}, u32[]{:S(2)}) %all-to-all-start) | async-done | bytes 147488 | tf_op jit(solution)/shard_map/all_to_all | solution.py:18
  35.6 0.2 convolution_convert_fusion.1
  35.9 0.7 copy.44
  36.6 0.0 copy-start.3
  36.6 0.0 copy-start.5
  36.6 3.7 %all-to-all-start.2 = ((bf16[8,96,96]{2,0,1:T(8,128)(2,1)}), bf16[8,96,96]{2,0,1:T(8,128)(2,1)S(1)}, u32[]{:S(2)}, u32[]{:S(2)}) async-start(bf16[8,96,96]{2,0,1:T(8,128)(2,1)} %copy.44), calls=%async_computation.2 | async-start | bytes 393216 | tf_op jit(solution)/shard_map/all_to_all | solution.py:35
  40.3 0.0 copy-done.1
  40.3 0.0 copy-done.7
  40.3 0.0 copy-done.9
  40.3 0.3 fusion.7
  40.7 0.0 copy-start.2
  40.7 0.0 copy-start.8
  40.7 8.5 %all-to-all-done.2 = bf16[8,96,96]{2,0,1:T(8,128)(2,1)S(1)} async-done(((bf16[8,96,96]{2,0,1:T(8,128)(2,1)}), bf16[8,96,96]{2,0,1:T(8,128)(2,1)S(1)}, u32[]{:S(2)}, u32[]{:S(2)}) %all-to-all-start.2) | async-done | bytes 147488 | tf_op jit(solution)/shard_map/all_to_all | solution.py:35
  49.2 0.1 fusion.39
  49.3 0.1 multiply_reduce_fusion.1
  49.4 0.0 copy-done.3
  49.4 0.0 copy-done.5
  49.4 0.4 fusion.60
  49.8 0.3 multiply_reduce_fusion.2
  50.1 0.0 copy-done.2
  50.1 0.0 copy-done.8
  50.1 0.4 convolution_bitcast_fusion
  50.5 0.2 fusion.26
  50.7 0.9 copy.47
  51.6 3.5 %all-to-all-start.3 = ((bf16[128,6,96]{2,1,0:T(8,128)(2,1)}), bf16[128,6,96]{2,1,0:T(8,128)(2,1)S(1)}, u32[]{:S(2)}, u32[]{:S(2)}) async-start(bf16[128,6,96]{2,1,0:T(8,128)(2,1)} %copy.47), calls=%async_computation.3 | async-start | bytes 524288 | tf_op jit(solution)/shard_map/all_to_all | solution.py:18
  55.1 0.9 copy.50
  56.0 9.1 %all-to-all-done.3 = bf16[128,6,96]{2,1,0:T(8,128)(2,1)S(1)} async-done(((bf16[128,6,96]{2,1,0:T(8,128)(2,1)}), bf16[128,6,96]{2,1,0:T(8,128)(2,1)S(1)}, u32[]{:S(2)}, u32[]{:S(2)}) %all-to-all-start.3) | async-done | bytes 147488 | tf_op jit(solution)/shard_map/all_to_all | solution.py:18
  65.1 3.5 %all-to-all-start.4 = ((bf16[128,6,96]{2,1,0:T(8,128)(2,1)}), bf16[128,6,96]{2,1,0:T(8,128)(2,1)S(1)}, u32[]{:S(2)}, u32[]{:S(2)}) async-start(bf16[128,6,96]{2,1,0:T(8,128)(2,1)} %copy.50), calls=%async_computation.4 | async-start | bytes 524288 | tf_op jit(solution)/shard_map/all_to_all | solution.py:19
  68.6 0.0 copy-start.10
  68.7 9.9 %all-to-all-done.4 = bf16[128,6,96]{2,1,0:T(8,128)(2,1)S(1)} async-done(((bf16[128,6,96]{2,1,0:T(8,128)(2,1)}), bf16[128,6,96]{2,1,0:T(8,128)(2,1)S(1)}, u32[]{:S(2)}, u32[]{:S(2)}) %all-to-all-start.4) | async-done | bytes 147488 | tf_op jit(solution)/shard_map/all_to_all | solution.py:19
  78.6 0.3 convolution_convert_fusion
  78.9 0.7 copy.55
  79.6 0.0 copy-start.4
  79.6 0.0 copy-start.6
  79.6 3.7 %all-to-all-start.5 = ((bf16[8,96,96]{2,0,1:T(8,128)(2,1)}), bf16[8,96,96]{2,0,1:T(8,128)(2,1)S(1)}, u32[]{:S(2)}, u32[]{:S(2)}) async-start(bf16[8,96,96]{2,0,1:T(8,128)(2,1)} %copy.55), calls=%async_computation.5 | async-start | bytes 393216 | tf_op jit(solution)/shard_map/all_to_all | solution.py:35
  83.3 0.0 copy-done.10
  83.3 0.3 fusion.4
  83.7 8.6 %all-to-all-done.5 = bf16[8,96,96]{2,0,1:T(8,128)(2,1)S(1)} async-done(((bf16[8,96,96]{2,0,1:T(8,128)(2,1)}), bf16[8,96,96]{2,0,1:T(8,128)(2,1)S(1)}, u32[]{:S(2)}, u32[]{:S(2)}) %all-to-all-start.5) | async-done | bytes 147488 | tf_op jit(solution)/shard_map/all_to_all | solution.py:35
  92.2 0.1 fusion.41
  92.3 0.1 multiply_reduce_fusion
  92.4 0.0 copy-done.4
  92.4 0.0 copy-done.6
  92.4 1.0 %fusion.10 = bf16[6,96,128]{2,1,0:T(8,128)(2,1)} fusion(f32[6,96,128]{2,1,0:T(8,128)S(1)} %get-tuple-element.10, f32[6,96,128]{2,1,0:T(8,128)S(1)} %fusion.4, f32[128]{0:T(128)S(1)} %copy-done.6, f32[6,96]{1,0:T(8,128)S(1)} %add_rsqrt_fusion, f32[6,96]{1,0:T(8,128)S(1)} %broadcast_multiply_fusion, bf16[128,128]{1,0:T(8,128)(2,1)S(1)} %copy-done.4, ...), kind=kOutput, calls=%fused_computation.18 | convolution fusion | flops 19464192 | bytes 922624 | tf_op jit(solution)/shard_map/krn,kc->rnc/dot_general | solution.py:42
  (12 shorter events, 0.2 us)
Async XLA Ops:
  0.0 2.3 %copy-start = (bf16[128,512]{1,0:T(8,128)(2,1)S(1)}, bf16[128,512]{1,0:T(8,128)(2,1)}, u32[]{:S(2)}) copy-start(bf16[128,512]{1,0:T(8,128)(2,1)} %param.13) | copy-start | bytes 393220
  4.6 17.4 %all-to-all-start.1 = ((bf16[128,6,96]{2,1,0:T(8,128)(2,1)}), bf16[128,6,96]{2,1,0:T(8,128)(2,1)S(1)}, u32[]{:S(2)}, u32[]{:S(2)}) async-start(bf16[128,6,96]{2,1,0:T(8,128)(2,1)} %copy.39), calls=%async_computation.1 | async-start | bytes 524288 | tf_op jit(solution)/shard_map/all_to_all | solution.py:19
  22.1 13.5 %all-to-all-start = ((bf16[128,6,96]{2,1,0:T(8,128)(2,1)}), bf16[128,6,96]{2,1,0:T(8,128)(2,1)S(1)}, u32[]{:S(2)}, u32[]{:S(2)}) async-start(bf16[128,6,96]{2,1,0:T(8,128)(2,1)} %copy.36), calls=%async_computation | async-start | bytes 524288 | tf_op jit(solution)/shard_map/all_to_all | solution.py:18
  25.6 14.7 %copy-start.1 = (bf16[6,96,128]{2,1,0:T(8,128)(2,1)S(1)}, bf16[6,96,128]{2,1,0:T(8,128)(2,1)}, u32[]{:S(2)}) copy-start(bf16[6,96,128]{2,1,0:T(8,128)(2,1)} %param.11) | copy-start | bytes 442372
  25.6 14.7 %copy-start.7 = (f32[128]{0:T(128)S(1)}, f32[128]{0:T(128)}, u32[]{:S(2)}) copy-start(f32[128]{0:T(128)} %param.12) | copy-start | bytes 1540
  25.6 14.7 %copy-start.9 = (bf16[128,128]{1,0:T(8,128)(2,1)S(1)}, bf16[128,128]{1,0:T(8,128)(2,1)}, u32[]{:S(2)}) copy-start(bf16[128,128]{1,0:T(8,128)(2,1)} %param.14) | copy-start | bytes 98308
  36.6 12.8 %copy-start.3 = (bf16[128,128]{1,0:T(8,128)(2,1)S(1)}, bf16[128,128]{1,0:T(8,128)(2,1)}, u32[]{:S(2)}) copy-start(bf16[128,128]{1,0:T(8,128)(2,1)} %param.16) | copy-start | bytes 98308
  36.6 12.8 %copy-start.5 = (f32[128]{0:T(128)S(1)}, f32[128]{0:T(128)}, u32[]{:S(2)}) copy-start(f32[128]{0:T(128)} %param.15) | copy-start | bytes 1540
  36.6 12.6 %all-to-all-start.2 = ((bf16[8,96,96]{2,0,1:T(8,128)(2,1)}), bf16[8,96,96]{2,0,1:T(8,128)(2,1)S(1)}, u32[]{:S(2)}, u32[]{:S(2)}) async-start(bf16[8,96,96]{2,0,1:T(8,128)(2,1)} %copy.44), calls=%async_computation.2 | async-start | bytes 393216 | tf_op jit(solution)/shard_map/all_to_all | solution.py:35
  40.7 9.5 %copy-start.2 = (bf16[128,512]{1,0:T(8,128)(2,1)S(1)}, bf16[128,512]{1,0:T(8,128)(2,1)}, u32[]{:S(2)}) copy-start(bf16[128,512]{1,0:T(8,128)(2,1)} %param.18) | copy-start | bytes 393220
  40.7 9.5 %copy-start.8 = (f32[128]{0:T(128)S(1)}, f32[128]{0:T(128)}, u32[]{:S(2)}) copy-start(f32[128]{0:T(128)} %param.17) | copy-start | bytes 1540
  51.6 13.5 %all-to-all-start.3 = ((bf16[128,6,96]{2,1,0:T(8,128)(2,1)}), bf16[128,6,96]{2,1,0:T(8,128)(2,1)S(1)}, u32[]{:S(2)}, u32[]{:S(2)}) async-start(bf16[128,6,96]{2,1,0:T(8,128)(2,1)} %copy.47), calls=%async_computation.3 | async-start | bytes 524288 | tf_op jit(solution)/shard_map/all_to_all | solution.py:18
  65.1 13.5 %all-to-all-start.4 = ((bf16[128,6,96]{2,1,0:T(8,128)(2,1)}), bf16[128,6,96]{2,1,0:T(8,128)(2,1)S(1)}, u32[]{:S(2)}, u32[]{:S(2)}) async-start(bf16[128,6,96]{2,1,0:T(8,128)(2,1)} %copy.50), calls=%async_computation.4 | async-start | bytes 524288 | tf_op jit(solution)/shard_map/all_to_all | solution.py:19
  68.6 14.7 %copy-start.10 = (bf16[128,128]{1,0:T(8,128)(2,1)S(1)}, bf16[128,128]{1,0:T(8,128)(2,1)}, u32[]{:S(2)}) copy-start(bf16[128,128]{1,0:T(8,128)(2,1)} %param.19) | copy-start | bytes 98308
  79.6 12.8 %copy-start.4 = (bf16[128,128]{1,0:T(8,128)(2,1)S(1)}, bf16[128,128]{1,0:T(8,128)(2,1)}, u32[]{:S(2)}) copy-start(bf16[128,128]{1,0:T(8,128)(2,1)} %param.21) | copy-start | bytes 98308
  79.6 12.8 %copy-start.6 = (f32[128]{0:T(128)S(1)}, f32[128]{0:T(128)}, u32[]{:S(2)}) copy-start(f32[128]{0:T(128)} %param.20) | copy-start | bytes 1540
  79.6 12.6 %all-to-all-start.5 = ((bf16[8,96,96]{2,0,1:T(8,128)(2,1)}), bf16[8,96,96]{2,0,1:T(8,128)(2,1)S(1)}, u32[]{:S(2)}, u32[]{:S(2)}) async-start(bf16[8,96,96]{2,0,1:T(8,128)(2,1)} %copy.55), calls=%async_computation.5 | async-start | bytes 393216 | tf_op jit(solution)/shard_map/all_to_all | solution.py:35
where the time goes:
time: 94.3 us; the launch traced here: 93.4 us
  waiting for transfers between devices  55.1 us (58%)
  starting transfers between devices  25.3 us (27%)
  local copies, waits for them, and re-layouts  5.17 us (5%)
  matrix products  4.23 us (4%)
  other arithmetic  3.23 us (3%)
    all_to_all x2, waiting for transfers between devices, channel_product(): lax.all_to_all(right_side, 'axial', split_axis=0, concat_axis=1, tiled=True)  19.1 us
    all_to_all x2, waiting for transfers between devices, channel_product(): lax.all_to_all(left_side, 'axial', split_axis=0, concat_axis=1, tiled=True)  19 us
    all_to_all x2, waiting for transfers between devices, update(): lax.all_to_all(product.astype(jnp.bfloat16), 'axial', split_axis=1, conca...  17.1 us
    all_to_all x2, starting transfers between devices, channel_product(): lax.all_to_all(right_side, 'axial', split_axis=0, concat_axis=1, tiled=True)  10.9 us
    all_to_all x2, starting transfers between devices, update(): lax.all_to_all(product.astype(jnp.bfloat16), 'axial', split_axis=1, conca...  7.31 us
    all_to_all x2, starting transfers between devices, channel_product(): lax.all_to_all(left_side, 'axial', split_axis=0, concat_axis=1, tiled=True)  7.06 us
  transfers between devices with their start and end apart: 6, of which 6 were waited for; matrix products, arithmetic and copies ran while one was open for 3% of the time, Pallas kernels for 0%

commit v1 on v0

--- a/solution.py
+++ b/solution.py
@@ -15,7 +15,12 @@
 def channel_product(left_side, right_side, outgoing):
     formula = "kil,kjl->kij" if outgoing else "kli,klj->kij"
     got_left, got_right = (
-        lax.all_to_all(left_side, "axial", split_axis=0, concat_axis=1, tiled=True),
+        jnp.concatenate(
+            lax.all_to_all(
+                jnp.stack(jnp.split(left_side, lax.axis_size("axial"), axis=0)), "axial", 0, 0
+            ),
+            axis=1,
+        ),
         lax.all_to_all(right_side, "axial", split_axis=0, concat_axis=1, tiled=True),
     )
     return jnp.einsum(formula, got_left, got_right, preferred_element_type=jnp.float32)

time: 94.3 us -> 101 us (1.071)
  local copies, waits for them, and re-layouts: 5.17 us -> 27.5 us
  waiting for transfers between devices: 55.1 us -> 35.7 us
  starting transfers between devices: 25.3 us -> 29.5 us
    all_to_all x2, waiting for transfers between devices: 19.1 us -> 0.75 us  [channel_product(): lax.all_to_all(right_side, 'axial', split_axis=0, concat_axis=1, tiled=True)]
    unnamed x22 -> x52, local copies, waits for them, and re-layouts: 0.06 us -> 18.1 us
    another operation x0 -> x36, local copies, waits for them, and re-layouts: none -> 6 us  [channel_product(): jnp.stack(jnp.split(left_side, lax.axis_size('axial'), axis=0))]
    all_to_all x2, starting transfers between devices: 7.06 us -> 11.2 us  [channel_product(): lax.all_to_all(jnp.stack(jnp.split(left_side, lax.axis_size('axial'), axi...]
    convert_element_type x2 -> x0, local copies, waits for them, and re-layouts: 1.77 us -> none  [update(): (jax.nn.sigmoid(projected[hidden:2 * hidden]) * projected[:hidden]).astyp...]
    all_to_all x2, waiting for transfers between devices: 19 us -> 17.8 us  [channel_product(): lax.all_to_all(jnp.stack(jnp.split(left_side, lax.axis_size('axial'), axi...]
  transfers between devices with their start and end apart: 6 -> 6, of which waited for: 6 -> 5; matrix products, arithmetic and copies ran while one was open for 3% -> 22% of each run, Pallas kernels for 0% -> 0%
where the time goes in v1:
time: 101 us; the launch traced here: 100 us
  waiting for transfers between devices  35.7 us (35%)
  starting transfers between devices  29.5 us (29%)
  local copies, waits for them, and re-layouts  27.5 us (27%)
  matrix products  4.23 us (4%)
  other arithmetic  3.23 us (3%)
    unnamed x52, local copies, waits for them, and re-layouts  18.1 us
    all_to_all x2, waiting for transfers between devices, channel_product(): lax.all_to_all(jnp.stack(jnp.split(left_side, lax.axis_size('axial'), axi...  17.8 us
    all_to_all x2, waiting for transfers between devices, update(): lax.all_to_all(product.astype(jnp.bfloat16), 'axial', split_axis=1, conca...  17.1 us
    all_to_all x2, starting transfers between devices, channel_product(): lax.all_to_all(jnp.stack(jnp.split(left_side, lax.axis_size('axial'), axi...  11.2 us
    all_to_all x2, starting transfers between devices, channel_product(): lax.all_to_all(right_side, 'axial', split_axis=0, concat_axis=1, tiled=True)  10.9 us
    all_to_all x2, starting transfers between devices, update(): lax.all_to_all(product.astype(jnp.bfloat16), 'axial', split_axis=1, conca...  7.31 us
    another operation x36, local copies, waits for them, and re-layouts, channel_product(): jnp.stack(jnp.split(left_side, lax.axis_size('axial'), axis=0))  6 us
  transfers between devices with their start and end apart: 6, of which 5 were waited for; matrix products, arithmetic and copies ran while one was open for 22% of the time, Pallas kernels for 0%

profile of v1, /device:TPU:0, one launch (start us, length us, event | category | flops | bytes accessed | tf_op | source)
XLA Modules:
  0.0 100.4 jit_solution(4192014433502394137)
XLA Ops:
  0.0 1.1 %convert_reduce_fusion = f32[6,96]{1,0:T(8,128)S(1)} fusion(bf16[6,96,128]{2,1,0:T(8,128)(2,1)} %param.11), kind=kLoop, calls=%fused_computation.20 | loop fusion | flops 146880 | bytes 149760 | tf_op jit(solution)/shard_map/reduce_sum | solution.py:10
  1.1 1.2 %fusion.19 = f32[6,96]{1,0:T(8,128)S(1)} fusion(bf16[6,96,128]{2,1,0:T(8,128)(2,1)} %param.11, f32[6,96]{1,0:T(8,128)S(1)} %broadcast_multiply_fusion.3), kind=kLoop, calls=%fused_computation.35 | loop fusion | flops 294336 | bytes 152064 | tf_op jit(solution)/shard_map/reduce_sum | solution.py:11
  2.3 1.3 %convolution_bitcast_fusion.1 = f32[512,6,96]{0,2,1:T(8,128)S(1)} fusion(bf16[128,512]{1,0:T(8,128)(2,1)S(1)} %copy-done, bf16[6,96,128]{2,1,0:T(8,128)(2,1)} %param.11, f32[128]{0:T(128)} %param.12, f32[6,96]{1,0:T(8,128)S(1)} %add_rsqrt_fusion.3, f32[6,96]{1,0:T(8,128)S(1)} %broadcast_multiply_fusion.3), kind=kOutput, calls=%fused_computation.1 | convolution fusion | flops 75866112 | bytes 1463296 | tf_op jit(solution)/shard_map/rnc,ck->krn/dot_general | solution.py:31
  3.6 0.2 fusion.34
  3.8 0.9 copy.96
  4.6 7.4 %all-to-all-start.1 = ((bf16[128,6,96]{2,1,0:T(8,128)(2,1)}), bf16[128,6,96]{2,1,0:T(8,128)(2,1)S(1)}, u32[]{:S(2)}, u32[]{:S(2)}) async-start(bf16[128,6,96]{2,1,0:T(8,128)(2,1)} %copy.96), calls=%async_computation.1 | async-start | bytes 524288 | tf_op jit(solution)/shard_map/all_to_all | solution.py:24
  12.0 0.6 slice_bitcast_fusion.16
  12.8 0.6 constant_dynamic-update-slice_fusion.15
  13.7 0.1 copy.84
  13.8 0.1 copy.85
  14.9 0.6 constant_dynamic-update-slice_fusion.14
  15.5 0.6 constant_dynamic-update-slice_fusion.13
  16.1 0.6 constant_dynamic-update-slice_fusion.12
  16.7 0.6 constant_dynamic-update-slice_fusion.11
  17.3 0.6 constant_dynamic-update-slice_fusion.10
  17.9 0.6 constant_dynamic-update-slice_fusion.9
  18.5 0.6 constant_dynamic-update-slice_fusion.8
  19.1 0.6 constant_dynamic-update-slice_fusion.7
  19.7 0.6 constant_dynamic-update-slice_fusion.6
  20.3 0.6 constant_dynamic-update-slice_fusion.5
  20.9 0.6 constant_dynamic-update-slice_fusion.4
  21.5 0.6 constant_dynamic-update-slice_fusion.3
  22.1 0.6 constant_dynamic-update-slice_fusion.2
  22.9 0.6 constant_dynamic-update-slice_fusion.1
  23.6 0.6 constant_dynamic-update-slice_fusion
  24.1 6.0 %all-to-all-start = ((bf16[16,8,6,96]{3,1,2,0:T(8,128)(2,1)}), bf16[16,8,6,96]{3,1,2,0:T(8,128)(2,1)S(1)}, u32[]{:S(2)}, u32[]{:S(2)}) async-start(bf16[16,8,6,96]{3,1,2,0:T(8,128)(2,1)} %constant_dynamic-update-slice_fusion), calls=%async_computation | async-start | bytes 393216 | tf_op jit(solution)/shard_map/all_to_all | solution.py:19
  30.2 8.9 %all-to-all-done = bf16[16,8,6,96]{3,1,2,0:T(8,128)(2,1)S(1)} async-done(((bf16[16,8,6,96]{3,1,2,0:T(8,128)(2,1)}), bf16[16,8,6,96]{3,1,2,0:T(8,128)(2,1)S(1)}, u32[]{:S(2)}, u32[]{:S(2)}) %all-to-all-start) | async-done | bytes 147488 | tf_op jit(solution)/shard_map/all_to_all | solution.py:19
  39.1 0.2 convolution_convert_fusion.1
  39.4 0.8 copy.101
  40.1 3.7 %all-to-all-start.2 = ((bf16[8,96,96]{2,0,1:T(8,128)(2,1)}), bf16[8,96,96]{2,0,1:T(8,128)(2,1)S(1)}, u32[]{:S(2)}, u32[]{:S(2)}) async-start(bf16[8,96,96]{2,0,1:T(8,128)(2,1)} %copy.101), calls=%async_computation.2 | async-start | bytes 393216 | tf_op jit(solution)/shard_map/all_to_all | solution.py:40
  43.8 0.3 fusion.7
  44.2 8.5 %all-to-all-done.2 = bf16[8,96,96]{2,0,1:T(8,128)(2,1)S(1)} async-done(((bf16[8,96,96]{2,0,1:T(8,128)(2,1)}), bf16[8,96,96]{2,0,1:T(8,128)(2,1)S(1)}, u32[]{:S(2)}, u32[]{:S(2)}) %all-to-all-start.2) | async-done | bytes 147488 | tf_op jit(solution)/shard_map/all_to_all | solution.py:40
  52.9 0.4 fusion.60
  53.3 0.3 multiply_reduce_fusion.2
  53.7 0.4 convolution_bitcast_fusion
  54.0 0.2 fusion.26
  54.2 0.6 slice_bitcast_fusion
  55.0 0.6 constant_dynamic-update-slice_fusion.31
  57.1 0.9 copy.120
  57.9 3.5 %all-to-all-start.4 = ((bf16[128,6,96]{2,1,0:T(8,128)(2,1)}), bf16[128,6,96]{2,1,0:T(8,128)(2,1)S(1)}, u32[]{:S(2)}, u32[]{:S(2)}) async-start(bf16[128,6,96]{2,1,0:T(8,128)(2,1)} %copy.120), calls=%async_computation.4 | async-start | bytes 524288 | tf_op jit(solution)/shard_map/all_to_all | solution.py:24
  61.5 0.6 constant_dynamic-update-slice_fusion.30
  62.1 0.6 constant_dynamic-update-slice_fusion.29
  62.7 0.6 constant_dynamic-update-slice_fusion.28
  63.3 0.6 constant_dynamic-update-slice_fusion.27
  63.9 0.6 constant_dynamic-update-slice_fusion.26
  64.5 0.6 constant_dynamic-update-slice_fusion.25
  65.1 0.6 constant_dynamic-update-slice_fusion.24
  65.7 0.6 constant_dynamic-update-slice_fusion.23
  66.3 0.6 constant_dynamic-update-slice_fusion.22
  66.9 0.6 constant_dynamic-update-slice_fusion.21
  67.5 0.6 constant_dynamic-update-slice_fusion.20
  68.1 0.6 constant_dynamic-update-slice_fusion.19
  68.7 0.6 constant_dynamic-update-slice_fusion.18
  69.5 0.6 constant_dynamic-update-slice_fusion.17
  70.1 0.6 constant_dynamic-update-slice_fusion.16
  70.7 0.7 all-to-all-done.4
  71.5 5.2 %all-to-all-start.3 = ((bf16[16,8,6,96]{3,1,2,0:T(8,128)(2,1)}), bf16[16,8,6,96]{3,1,2,0:T(8,128)(2,1)S(1)}, u32[]{:S(2)}, u32[]{:S(2)}) async-start(bf16[16,8,6,96]{3,1,2,0:T(8,128)(2,1)} %constant_dynamic-update-slice_fusion.16), calls=%async_computation.3 | async-start | bytes 393216 | tf_op jit(solution)/shard_map/all_to_all | solution.py:19
  76.7 8.9 %all-to-all-done.3 = bf16[16,8,6,96]{3,1,2,0:T(8,128)(2,1)S(1)} async-done(((bf16[16,8,6,96]{3,1,2,0:T(8,128)(2,1)}), bf16[16,8,6,96]{3,1,2,0:T(8,128)(2,1)S(1)}, u32[]{:S(2)}, u32[]{:S(2)}) %all-to-all-start.3) | async-done | bytes 147488 | tf_op jit(solution)/shard_map/all_to_all | solution.py:19
  85.7 0.2 convolution_convert_fusion
  85.9 0.8 copy.125
  86.7 3.7 %all-to-all-start.5 = ((bf16[8,96,96]{2,0,1:T(8,128)(2,1)}), bf16[8,96,96]{2,0,1:T(8,128)(2,1)S(1)}, u32[]{:S(2)}, u32[]{:S(2)}) async-start(bf16[8,96,96]{2,0,1:T(8,128)(2,1)} %copy.125), calls=%async_computation.5 | async-start | bytes 393216 | tf_op jit(solution)/shard_map/all_to_all | solution.py:40
  90.3 0.3 fusion.4
  90.7 8.6 %all-to-all-done.5 = bf16[8,96,96]{2,0,1:T(8,128)(2,1)S(1)} async-done(((bf16[8,96,96]{2,0,1:T(8,128)(2,1)}), bf16[8,96,96]{2,0,1:T(8,128)(2,1)S(1)}, u32[]{:S(2)}, u32[]{:S(2)}) %all-to-all-start.5) | async-done | bytes 147488 | tf_op jit(solution)/shard_map/all_to_all | solution.py:40
  99.4 1.0 fusion.10
  (67 shorter events, 3.7 us)
Async XLA Ops:
  0.0 2.3 %copy-start = (bf16[128,512]{1,0:T(8,128)(2,1)S(1)}, bf16[128,512]{1,0:T(8,128)(2,1)}, u32[]{:S(2)}) copy-start(bf16[128,512]{1,0:T(8,128)(2,1)} %param.13) | copy-start | bytes 393220
  4.6 19.5 %all-to-all-start.1 = ((bf16[128,6,96]{2,1,0:T(8,128)(2,1)}), bf16[128,6,96]{2,1,0:T(8,128)(2,1)S(1)}, u32[]{:S(2)}, u32[]{:S(2)}) async-start(bf16[128,6,96]{2,1,0:T(8,128)(2,1)} %copy.96), calls=%async_computation.1 | async-start | bytes 524288 | tf_op jit(solution)/shard_map/all_to_all | solution.py:24
  22.9 20.9 %copy-start.1 = (bf16[6,96,128]{2,1,0:T(8,128)(2,1)S(1)}, bf16[6,96,128]{2,1,0:T(8,128)(2,1)}, u32[]{:S(2)}) copy-start(bf16[6,96,128]{2,1,0:T(8,128)(2,1)} %param.11) | copy-start | bytes 442372
  22.9 20.9 %copy-start.7 = (f32[128]{0:T(128)S(1)}, f32[128]{0:T(128)}, u32[]{:S(2)}) copy-start(f32[128]{0:T(128)} %param.12) | copy-start | bytes 1540
  22.9 20.9 %copy-start.9 = (bf16[128,128]{1,0:T(8,128)(2,1)S(1)}, bf16[128,128]{1,0:T(8,128)(2,1)}, u32[]{:S(2)}) copy-start(bf16[128,128]{1,0:T(8,128)(2,1)} %param.14) | copy-start | bytes 98308
  24.1 15.0 %all-to-all-start = ((bf16[16,8,6,96]{3,1,2,0:T(8,128)(2,1)}), bf16[16,8,6,96]{3,1,2,0:T(8,128)(2,1)S(1)}, u32[]{:S(2)}, u32[]{:S(2)}) async-start(bf16[16,8,6,96]{3,1,2,0:T(8,128)(2,1)} %constant_dynamic-update-slice_fusion), calls=%async_computation | async-start | bytes 393216 | tf_op jit(solution)/shard_map/all_to_all | solution.py:19
  40.1 12.8 %copy-start.3 = (bf16[128,128]{1,0:T(8,128)(2,1)S(1)}, bf16[128,128]{1,0:T(8,128)(2,1)}, u32[]{:S(2)}) copy-start(bf16[128,128]{1,0:T(8,128)(2,1)} %param.16) | copy-start | bytes 98308
  40.1 12.8 %copy-start.5 = (f32[128]{0:T(128)S(1)}, f32[128]{0:T(128)}, u32[]{:S(2)}) copy-start(f32[128]{0:T(128)} %param.15) | copy-start | bytes 1540
  40.1 12.6 %all-to-all-start.2 = ((bf16[8,96,96]{2,0,1:T(8,128)(2,1)}), bf16[8,96,96]{2,0,1:T(8,128)(2,1)S(1)}, u32[]{:S(2)}, u32[]{:S(2)}) async-start(bf16[8,96,96]{2,0,1:T(8,128)(2,1)} %copy.101), calls=%async_computation.2 | async-start | bytes 393216 | tf_op jit(solution)/shard_map/all_to_all | solution.py:40
  44.2 9.5 %copy-start.2 = (bf16[128,512]{1,0:T(8,128)(2,1)S(1)}, bf16[128,512]{1,0:T(8,128)(2,1)}, u32[]{:S(2)}) copy-start(bf16[128,512]{1,0:T(8,128)(2,1)} %param.18) | copy-start | bytes 393220
  44.2 9.5 %copy-start.8 = (f32[128]{0:T(128)S(1)}, f32[128]{0:T(128)}, u32[]{:S(2)}) copy-start(f32[128]{0:T(128)} %param.17) | copy-start | bytes 1540
  57.9 13.5 %all-to-all-start.4 = ((bf16[128,6,96]{2,1,0:T(8,128)(2,1)}), bf16[128,6,96]{2,1,0:T(8,128)(2,1)S(1)}, u32[]{:S(2)}, u32[]{:S(2)}) async-start(bf16[128,6,96]{2,1,0:T(8,128)(2,1)} %copy.120), calls=%async_computation.4 | async-start | bytes 524288 | tf_op jit(solution)/shard_map/all_to_all | solution.py:24
  69.5 20.9 %copy-start.10 = (bf16[128,128]{1,0:T(8,128)(2,1)S(1)}, bf16[128,128]{1,0:T(8,128)(2,1)}, u32[]{:S(2)}) copy-start(bf16[128,128]{1,0:T(8,128)(2,1)} %param.19) | copy-start | bytes 98308
  71.5 14.2 %all-to-all-start.3 = ((bf16[16,8,6,96]{3,1,2,0:T(8,128)(2,1)}), bf16[16,8,6,96]{3,1,2,0:T(8,128)(2,1)S(1)}, u32[]{:S(2)}, u32[]{:S(2)}) async-start(bf16[16,8,6,96]{3,1,2,0:T(8,128)(2,1)} %constant_dynamic-update-slice_fusion.16), calls=%async_computation.3 | async-start | bytes 393216 | tf_op jit(solution)/shard_map/all_to_all | solution.py:19
  86.7 12.8 %copy-start.4 = (bf16[128,128]{1,0:T(8,128)(2,1)S(1)}, bf16[128,128]{1,0:T(8,128)(2,1)}, u32[]{:S(2)}) copy-start(bf16[128,128]{1,0:T(8,128)(2,1)} %param.21) | copy-start | bytes 98308
  86.7 12.8 %copy-start.6 = (f32[128]{0:T(128)S(1)}, f32[128]{0:T(128)}, u32[]{:S(2)}) copy-start(f32[128]{0:T(128)} %param.20) | copy-start | bytes 1540
  86.7 12.6 %all-to-all-start.5 = ((bf16[8,96,96]{2,0,1:T(8,128)(2,1)}), bf16[8,96,96]{2,0,1:T(8,128)(2,1)S(1)}, u32[]{:S(2)}, u32[]{:S(2)}) async-start(bf16[8,96,96]{2,0,1:T(8,128)(2,1)} %copy.125), calls=%async_computation.5 | async-start | bytes 393216 | tf_op jit(solution)/shard_map/all_to_all | solution.py:40
